TPU v7x, 32 devices: a whole 2x2x4 slice. The times are simulated.
32 devices in a mesh: grp: 2 (over x), slab: 16 (over z, y, core).
Axes of the slice: x: 2, y: 2, z: 4, core: 2. Of those that a mesh axis runs over, the one named last changes fastest.
Arguments:
- volume: bfloat16 [64, 1024, 1024], P(('grp', 'slab')), parts along dimension 0, may hold values from -60 to 60
- plane_shift: int32 [4, 32], P('grp', 'slab'), parts along dimension 0, may hold values from -64 to 64
- plane_weight: float32 [4, 32], P('grp', 'slab'), parts along dimension 0, may hold values from 0 to 1
- column_left: int32 [4, 1024], P('grp'), parts along dimension 0, may hold values from 0 to 1022
- column_weight: float32 [4, 1024], P('grp'), parts along dimension 0, may hold values from 0 to 1
- window_center: int32 [4, 2], P('grp'), parts along dimension 0, may hold values from -200 to 199
- tilt_owner: int32 [32], P('grp'), parts along dimension 0, may hold values from 0 to 15, each once
- reference_band: float32 [32, 2, 128, 128], P(('grp', 'slab')), parts along dimension 0, may hold values from -6 to 6
Outputs:
- correlation: float32 [4, 16, 128], P('grp', 'slab'), parts along dimension 0
- peaks: float32 [4], P('grp'), parts along dimension 0
There are 2 independent parts, one for each index of `grp`. A program takes and returns all parts, laid end to end along the dimension named above; each array names one. Nothing has to cross between parts.
Inputs may be any that keep to these rules, and one draw needn't show every extreme that they name: `tilt_owner`: the first 2 entries name the owners of the tilts, one slab index each.
All inputs are finite; a program needn't handle non-finite values.
Results may differ from a plain program's by a relative error of at most 0.0003.
Values sent between devices are 32-bit elements; how exact they have to be, the bound alone decides.
A program may use at most 128 MiB of HBM per device.

v0:
```python
import math
import jax
import jax.numpy as jnp
from jax import lax
from jax.sharding import PartitionSpec as P

Y = 1024
X = 1024
BAND = 128
WIN_COLS = 128
TILTS = 2
WIN_ROWS_DEV = 1


def from_root(value, axis, source):
    kept = jnp.where(lax.axis_index(axis) == source, value, 0).astype(value.dtype)
    return lax.psum(kept, axis)


def phase_pair(left_ints, right_ints, length):
    product = left_ints[:, None] * right_ints[None, :] % length
    angle = product.astype(jnp.float32) * (2.0 * math.pi / length)
    return (jnp.cos(angle), jnp.sin(angle))


def matmul(first, second):
    return jnp.dot(
        first, second, precision=lax.Precision.HIGHEST, preferred_element_type=jnp.float32
    )


def reproject(volume, shifts, weights, left_cols, right_share, row_count):
    grid_width = volume.shape[2]
    margin = grid_width // 16 + 1
    padded_all = jnp.pad(volume, ((0, 0), (0, 0), (margin, margin)))
    summed = jnp.zeros((row_count, grid_width), jnp.float32)
    for plane_no in range(volume.shape[0]):
        padded = padded_all[plane_no]
        near_cells = lax.dynamic_slice_in_dim(
            padded, margin - shifts[plane_no], grid_width, 1
        ).astype(jnp.float32)
        far_cells = lax.dynamic_slice_in_dim(
            padded, margin - shifts[plane_no] - 1, grid_width, 1
        ).astype(jnp.float32)
        summed = summed + (1.0 - weights[plane_no]) * near_cells + weights[plane_no] * far_cells
    left_values = jnp.take(summed, left_cols, axis=1)
    right_values = jnp.take(summed, left_cols + 1, axis=1)
    return (1.0 - right_share) * left_values + right_share * right_values


def band_part(projected):
    row_count, grid_width = projected.shape
    freq_cols = jnp.arange(BAND, dtype=jnp.int32)
    freq_rows = freq_cols - BAND // 2
    col_cos, col_sin = phase_pair(jnp.arange(grid_width, dtype=jnp.int32), freq_cols, grid_width)
    real_half = matmul(projected, col_cos)
    imag_half = -matmul(projected, col_sin)
    row_ids = jnp.arange(row_count, dtype=jnp.int32)
    row_cos, row_sin = phase_pair(freq_rows, row_ids, Y)
    spec_real = matmul(row_cos, real_half) + matmul(row_sin, imag_half)
    spec_imag = matmul(row_cos, imag_half) - matmul(row_sin, real_half)
    return jnp.stack([spec_real, spec_imag])


def correlate(spectrum, owned, center, row_ids, total_rows):
    spec_real, spec_imag = (spectrum[0], spectrum[1])
    ref_real, ref_imag = (owned[0], owned[1])
    cross_real = spec_real * ref_real + spec_imag * ref_imag
    cross_imag = spec_imag * ref_real - spec_real * ref_imag
    energy_spec = jnp.mean(spec_real * spec_real + spec_imag * spec_imag) + 1e-06
    energy_ref = jnp.mean(ref_real * ref_real + ref_imag * ref_imag) + 1e-06
    freq_cols = jnp.arange(BAND, dtype=jnp.int32)
    freq_rows = freq_cols - BAND // 2
    offsets_y = center[0] + row_ids - total_rows // 2
    offsets_x = center[1] + jnp.arange(WIN_COLS, dtype=jnp.int32) - WIN_COLS // 2
    row_cos, row_sin = phase_pair(offsets_y, freq_rows, Y)
    col_cos, col_sin = phase_pair(freq_cols, offsets_x, X)
    half_real = matmul(row_cos, cross_real) - matmul(row_sin, cross_imag)
    half_imag = matmul(row_cos, cross_imag) + matmul(row_sin, cross_real)
    return (matmul(half_real, col_cos) - matmul(half_imag, col_sin)) / (
        BAND * jnp.sqrt(energy_spec * energy_ref)
    )


def per_device(
    volume,
    plane_shift,
    plane_weight,
    column_left,
    column_weight,
    window_center,
    tilt_owner,
    reference_band,
):
    devices = lax.axis_size("slab")
    position = lax.axis_index("slab")
    partials = []
    for which in range(TILTS):

        def rows_term(first_row, row_count, which=which):
            return reproject(
                volume,
                plane_shift[which],
                plane_weight[which],
                column_left[which],
                column_weight[which],
                row_count,
            )

        partials.append(band_part(rows_term(0, Y)))
    stacked = jnp.stack(partials)
    mine = reference_band[0]
    spectra = lax.psum(stacked, "slab")
    references = jnp.stack([from_root(mine, "slab", tilt_owner[which]) for which in range(TILTS)])
    total_rows = WIN_ROWS_DEV * devices
    outputs = []
    maxima = []
    row_ids = position * WIN_ROWS_DEV + jnp.arange(WIN_ROWS_DEV, dtype=jnp.int32)
    for which in range(TILTS):
        corr = correlate(
            spectra[which], references[which], window_center[which], row_ids, total_rows
        )
        outputs.append(corr)
        maxima.append(jnp.max(corr))
    peaks = lax.pmax(jnp.stack(maxima), "slab")
    return (jnp.stack(outputs), peaks)


def solution(mesh):
    placed = (
        P(("grp", "slab"), None, None),
        P("grp", "slab"),
        P("grp", "slab"),
        P("grp", None),
        P("grp", None),
        P("grp", None),
        P("grp"),
        P(("grp", "slab"), None, None, None),
    )
    return jax.shard_map(
        per_device,
        mesh=mesh,
        in_specs=placed,
        out_specs=(P("grp", "slab", None), P("grp")),
        check_vma=False,
    )
```

profile of v0, /device:TPU:0, one launch (start us, length us, event | category | flops | bytes accessed | tf_op | source)
XLA Modules:
  0.0 311.6 jit_solution(11527147601551082680)
XLA Ops:
  24.0 6.2 %copy.10 = bf16[2,1024,1024]{1,2,0:T(8,128)(2,1)} copy(bf16[2,1024,1024]{2,1,0:T(8,128)(2,1)} %param.10) | data formatting | bytes 8388608 | tf_op args[0]
  30.2 5.0 %pad_slice_fusion.1 = (bf16[1,1024,1154]{1,2,0:T(8,128)(2,1)S(1)}, bf16[1,1024,1154]{1,2,0:T(8,128)(2,1)}) fusion(bf16[2,1024,1024]{1,2,0:T(8,128)(2,1)} %copy.10), kind=kLoop, calls=%fused_computation.5 | loop fusion | bytes 8921088 | tf_op jit(solution)/shard_map/slice | solution.py:38
  35.2 12.6 %add_bitcast_fusion.1 = (f32[1024,1024]{0,1:T(8,128)}, f32[1024,1024]{0,1:T(8,128)}) fusion(bf16[1,1024,1154]{1,2,0:T(8,128)(2,1)} %get-tuple-element.11, s32[]{:T(128)S(6)} %select_n.127, f32[]{:T(128)} %bitcast.11, s32[]{:T(128)S(6)} %select_n.126, f32[]{:T(128)S(6)} %sub.140, bf16[1,1024,1154]{1,2,0:T(8,128)(2,1)S(1)} %get-tuple-element.10, ...), kind=kLoop, calls=%fused_computation.13 | loop fusion | flops 23068672 | bytes 25165888 | tf_op jit(solution)/shard_map/add | solution.py:45
  47.8 8.6 %gather_fusion.2 = f32[1024,1024]{1,0:T(8,128)} fusion(f32[1024,1024]{0,1:T(8,128)} %get-tuple-element.9, s32[1024]{0:T(1024)S(1)} %get-tuple-element.34), kind=kCustom, calls=%fused_computation.2.clone | custom fusion | bytes 8392704 | tf_op jit(solution)/shard_map/jit(_take)/gather | solution.py:46
  56.4 8.6 %gather_fusion.3 = f32[1024,1024]{1,0:T(8,128)} fusion(f32[1024,1024]{0,1:T(8,128)} %get-tuple-element.9, s32[1024]{0:T(1024)S(1)} %get-tuple-element.35), kind=kCustom, calls=%fused_computation.3.clone | custom fusion | bytes 8392704 | tf_op jit(solution)/shard_map/jit(_take)/gather | solution.py:47
  65.0 4.4 %fusion = f32[1024,1024]{0,1:T(8,128)S(1)} fusion(f32[1024,1024]{1,0:T(8,128)} %gather_fusion.3, f32[1024,1024]{1,0:T(8,128)} %gather_fusion.2, f32[1024]{0:T(1024)S(1)} %bitcast.250, f32[1024]{0:T(1024)S(1)} %bitcast.249, pred[1024]{0:T(1024)(128)(4,1)S(1)} %get-tuple-element.33, pred[1024]{0:T(1024)(128)(4,1)S(1)} %get-tuple-element.32), kind=kLoop, calls=%fused_computation.7 | loop fusion | flops 5242880 | bytes 12593152 | tf_op jit(solution)/shard_map/add | solution.py:48
  69.4 8.5 %fusion.32 = f32[1024,128]{1,0:T(8,128)S(1)} fusion(f32[1024,1024]{0,1:T(8,128)S(1)} %fusion), kind=kOutput, calls=%fused_computation.69 | convolution fusion | flops 1612447744 | bytes 4718592 | tf_op jit(solution)/shard_map/dot_general | solution.py:27
  77.9 21.3 %convolution_negate_fusion = f32[1024,128]{1,0:T(8,128)S(1)} fusion(f32[1024,1024]{0,1:T(8,128)S(1)} %fusion), kind=kOutput, calls=%fused_computation.14 | convolution fusion | flops 1612578816 | bytes 4718592 | tf_op jit(solution)/shard_map/dot_general | solution.py:27
  99.2 8.6 %gather_fusion = f32[1024,1024]{1,0:T(8,128)} fusion(f32[1024,1024]{0,1:T(8,128)} %get-tuple-element.8, s32[1024]{0:T(1024)S(1)} %get-tuple-element.30), kind=kCustom, calls=%fused_computation.clone | custom fusion | bytes 8392704 | tf_op jit(solution)/shard_map/jit(_take)/gather | solution.py:46
  107.8 8.6 %gather_fusion.1 = f32[1024,1024]{1,0:T(8,128)} fusion(f32[1024,1024]{0,1:T(8,128)} %get-tuple-element.8, s32[1024]{0:T(1024)S(1)} %get-tuple-element.31), kind=kCustom, calls=%fused_computation.1.clone | custom fusion | bytes 8392704 | tf_op jit(solution)/shard_map/jit(_take)/gather | solution.py:47
  116.4 4.0 %fusion.1 = f32[1024,1024]{0,1:T(8,128)S(1)} fusion(f32[1024,1024]{1,0:T(8,128)} %gather_fusion.1, f32[1024,1024]{1,0:T(8,128)} %gather_fusion, f32[1024]{0:T(1024)S(1)} %bitcast.248, f32[1024]{0:T(1024)S(1)} %bitcast.247, pred[1024]{0:T(1024)(128)(4,1)S(1)} %get-tuple-element.29, pred[1024]{0:T(1024)(128)(4,1)S(1)} %get-tuple-element.28), kind=kLoop, calls=%fused_computation.10 | loop fusion | flops 5242880 | bytes 12593152 | tf_op jit(solution)/shard_map/add | solution.py:48
  120.4 8.5 %fusion.34 = f32[1024,128]{1,0:T(8,128)S(1)} fusion(f32[1024,1024]{0,1:T(8,128)S(1)} %fusion.1), kind=kOutput, calls=%fused_computation.70 | convolution fusion | flops 1612447744 | bytes 4718592 | tf_op jit(solution)/shard_map/dot_general | solution.py:27
  128.9 8.9 %convolution_negate_fusion.1 = f32[1024,128]{1,0:T(8,128)S(1)} fusion(f32[1024,1024]{0,1:T(8,128)S(1)} %fusion.1), kind=kOutput, calls=%fused_computation.15 | convolution fusion | flops 1612578816 | bytes 4718592 | tf_op jit(solution)/shard_map/dot_general | solution.py:27
  137.9 3.0 fusion.42
  140.9 3.0 fusion.40
  143.9 3.0 fusion.3
  146.9 3.0 fusion.2
  149.9 3.0 fusion.46
  152.9 3.2 %fusion.44 = f32[128,128]{1,0:T(8,128)S(1)} fusion(f32[1024,128]{1,0:T(8,128)S(1)} %convolution_negate_fusion.1, s32[128]{0:T(128)S(1)} %iota_add_fusion), kind=kOutput, calls=%fused_computation.75 | convolution fusion | flops 203161600 | bytes 590336 | tf_op jit(solution)/shard_map/dot_general | solution.py:27
  156.1 3.0 fusion.5
  159.1 3.0 fusion.4
  168.7 91.1 %all-reduce.4.cloned.1.call-done = (f32[2,2,128,128]{3,2,1,0:T(8,128)}, f32[2,128,128]{2,1,0:T(8,128)}, f32[2,128,128]{2,1,0:T(8,128)}) async-done(((f32[2,2,128,128]{3,2,1,0:T(8,128)}, f32[2,128,128]{2,1,0:T(8,128)}, f32[2,128,128]{2,1,0:T(8,128)}), (f32[2,2,128,128]{3,2,1,0:T(8,128)}, f32[2,128,128]{2,1,0:T(8,128)}, f32[2,128,128]{2,1,0:T(8,128)})) %all-reduce.4.cloned.1.call-update) | async-done | bytes 524304 | tf_op jit(solution)/shard_map/psum | solution.py:113
  259.8 1.7 multiply_subtract_fusion.1
  271.8 32.3 %pmax.7 = f32[2]{0:T(128)} all-reduce(f32[2]{0:T(128)S(1)} %pad_maximum_fusion.2), channel_id=1, replica_groups=mesh['grp'=2,'slab'=16] {'slab'}, use_global_device_ids=true, to_apply=%region_9.11 | all-reduce | flops 2 | bytes 16 | tf_op jit(solution)/shard_map/pmax | solution.py:125
  (41 shorter events, 15.9 us)
Async XLA Ops:
  7.2 252.6 %all-reduce.4.cloned.1.call-start = ((), (), s32[]{:S(2)}) async-start(), calls=%async_computation | async-start | bytes 1048576 | tf_op jit(solution)/shard_map/psum | solution.py:113
  56.4 8.6 %copy-start.1 = (f32[2,1024]{1,0:T(2,128)S(1)}, f32[2,1024]{1,0:T(2,128)}, u32[]{:S(2)}) copy-start(f32[2,1024]{1,0:T(2,128)} %param.14) | copy-start | bytes 24580
  149.9 12.2 %copy-start.3 = (s32[16]{0:T(128)S(1)}, s32[16]{0:T(128)}, u32[]{:S(2)}) copy-start(s32[16]{0:T(128)} %param.16) | copy-start | bytes 196
  152.9 11.8 %copy-start = (f32[1,2,128,128]{3,2,1,0:T(8,128)S(1)}, f32[1,2,128,128]{3,2,1,0:T(8,128)}, u32[]{:S(2)}) copy-start(f32[1,2,128,128]{3,2,1,0:T(8,128)} %param.17) | copy-start | bytes 393220
  152.9 12.6 %copy-start.2 = (s32[2,2]{1,0:T(2,128)S(1)}, s32[2,2]{1,0:T(2,128)}, u32[]{:S(2)}) copy-start(s32[2,2]{1,0:T(2,128)} %param.15) | copy-start | bytes 52
Sparse Core Ops, SparseCore 0:
  165.6 94.1 all-reduce.3
where the time goes:
time: 318 us; the launch traced here: 312 us
  waiting for transfers between devices  91.1 us (29%)
  matrix products  75.9 us (24%)
  local copies, waits for them, and re-layouts  50.6 us (16%)
  between operations  32.7 us (10%)
  blocking collectives  32.3 us (10%)
  other arithmetic  29 us (9%)
    psum x1, waiting for transfers between devices, per_device(): spectra = lax.psum(stacked, 'slab')  91.1 us
    dot_general x24, matrix products, matmul(): jnp.dot(first, second, precision=lax.Precision.HIGHEST, preferred_element...  75.9 us
    pmax x1, blocking collectives, per_device(): peaks = lax.pmax(jnp.stack(maxima), 'slab')  32.3 us
    gather x2, local copies, waits for them, and re-layouts, reproject(): right_values = jnp.take(summed, left_cols + 1, axis=1)  17.2 us
    gather x2, local copies, waits for them, and re-layouts, reproject(): left_values = jnp.take(summed, left_cols, axis=1)  17.2 us
    add x1, other arithmetic, reproject(): summed + (1.0 - weights[plane_no]) * near_cells  12.6 us
    add x2, other arithmetic, reproject(): return (1.0 - right_share) * left_values + right_share * right_values  8.41 us
  transfers between devices with their start and end apart: 1, of which 1 were waited for; matrix products, arithmetic and copies ran while one was open for 1% of the time, Pallas kernels for 0%

commit v1 on v0

--- a/solution.py
+++ b/solution.py
@@ -10,6 +10,9 @@
 WIN_COLS = 128
 TILTS = 2
 WIN_ROWS_DEV = 1
+render_slices = lambda sheet, device_axis: jax.lax.all_gather(sheet, axis_name=device_axis).sum(
+    axis=0
+)
 
 
 def from_root(value, axis, source):
@@ -110,7 +113,7 @@
         partials.append(band_part(rows_term(0, Y)))
     stacked = jnp.stack(partials)
     mine = reference_band[0]
-    spectra = lax.psum(stacked, "slab")
+    spectra = render_slices(stacked, "slab")
     references = jnp.stack([from_root(mine, "slab", tilt_owner[which]) for which in range(TILTS)])
     total_rows = WIN_ROWS_DEV * devices
     outputs = []

time: 318 us -> 366 us (1.15)
  waiting for transfers between devices: 91.1 us -> 137 us
    all_gather x0 -> x1, waiting for transfers between devices: none -> 47.5 us  [jax.lax.all_gather(sheet, axis_name=device_axis).sum(axis=0)]
  transfers between devices with their start and end apart: 1 -> 2, of which waited for: 1 -> 2; matrix products, arithmetic and copies ran while one was open for 1% -> 2% of each run, Pallas kernels for 0% -> 0%
where the time goes in v1:
time: 366 us; the launch traced here: 360 us
  waiting for transfers between devices  137 us (37%)
  matrix products  75.9 us (21%)
  local copies, waits for them, and re-layouts  50.6 us (14%)
  between operations  32.7 us (9%)
  blocking collectives  32.4 us (9%)
  other arithmetic  31.2 us (9%)
    psum x1, waiting for transfers between devices, from_root(): return lax.psum(kept, axis)  89.5 us
    dot_general x24, matrix products, matmul(): jnp.dot(first, second, precision=lax.Precision.HIGHEST, preferred_element...  75.9 us
    all_gather x1, waiting for transfers between devices, jax.lax.all_gather(sheet, axis_name=device_axis).sum(axis=0)  47.5 us
    pmax x1, blocking collectives, per_device(): peaks = lax.pmax(jnp.stack(maxima), 'slab')  32.4 us
    gather x2, local copies, waits for them, and re-layouts, reproject(): right_values = jnp.take(summed, left_cols + 1, axis=1)  17.2 us
    gather x2, local copies, waits for them, and re-layouts, reproject(): left_values = jnp.take(summed, left_cols, axis=1)  17.2 us
    add x1, other arithmetic, reproject(): summed + (1.0 - weights[plane_no]) * near_cells  12.6 us
    add x2, other arithmetic, reproject(): return (1.0 - right_share) * left_values + right_share * right_values  8.41 us
  transfers between devices with their start and end apart: 2, of which 2 were waited for; matrix products, arithmetic and copies ran while one was open for 2% of the time, Pallas kernels for 0%

profile of v1, /device:TPU:0, one launch (start us, length us, event | category | flops | bytes accessed | tf_op | source)
XLA Modules:
  0.0 359.8 jit_solution(15411603438826924273)
XLA Ops:
  24.0 6.2 %copy.11 = bf16[2,1024,1024]{1,2,0:T(8,128)(2,1)} copy(bf16[2,1024,1024]{2,1,0:T(8,128)(2,1)} %param.10) | data formatting | bytes 8388608 | tf_op args[0]
  30.2 5.0 %pad_slice_fusion.1 = (bf16[1,1024,1154]{1,2,0:T(8,128)(2,1)S(1)}, bf16[1,1024,1154]{1,2,0:T(8,128)(2,1)}) fusion(bf16[2,1024,1024]{1,2,0:T(8,128)(2,1)} %copy.11), kind=kLoop, calls=%fused_computation.5 | loop fusion | bytes 8921088 | tf_op jit(solution)/shard_map/slice | solution.py:41
  35.2 12.6 %add_bitcast_fusion.1 = (f32[1024,1024]{0,1:T(8,128)}, f32[1024,1024]{0,1:T(8,128)}) fusion(bf16[1,1024,1154]{1,2,0:T(8,128)(2,1)} %get-tuple-element.10, s32[]{:T(128)S(6)} %select_n.127, f32[]{:T(128)} %bitcast.11, s32[]{:T(128)S(6)} %select_n.126, f32[]{:T(128)S(6)} %sub.140, bf16[1,1024,1154]{1,2,0:T(8,128)(2,1)S(1)} %get-tuple-element.9, ...), kind=kLoop, calls=%fused_computation.13 | loop fusion | flops 23068672 | bytes 25165888 | tf_op jit(solution)/shard_map/add | solution.py:48
  47.8 8.6 %gather_fusion.2 = f32[1024,1024]{1,0:T(8,128)} fusion(f32[1024,1024]{0,1:T(8,128)} %get-tuple-element.8, s32[1024]{0:T(1024)S(1)} %get-tuple-element.33), kind=kCustom, calls=%fused_computation.2.clone | custom fusion | bytes 8392704 | tf_op jit(solution)/shard_map/jit(_take)/gather | solution.py:49
  56.4 8.6 %gather_fusion.3 = f32[1024,1024]{1,0:T(8,128)} fusion(f32[1024,1024]{0,1:T(8,128)} %get-tuple-element.8, s32[1024]{0:T(1024)S(1)} %get-tuple-element.34), kind=kCustom, calls=%fused_computation.3.clone | custom fusion | bytes 8392704 | tf_op jit(solution)/shard_map/jit(_take)/gather | solution.py:50
  65.0 4.4 %fusion = f32[1024,1024]{0,1:T(8,128)S(1)} fusion(f32[1024,1024]{1,0:T(8,128)} %gather_fusion.3, f32[1024,1024]{1,0:T(8,128)} %gather_fusion.2, f32[1024]{0:T(1024)S(1)} %bitcast.252, f32[1024]{0:T(1024)S(1)} %bitcast.251, pred[1024]{0:T(1024)(128)(4,1)S(1)} %get-tuple-element.32, pred[1024]{0:T(1024)(128)(4,1)S(1)} %get-tuple-element.31), kind=kLoop, calls=%fused_computation.7 | loop fusion | flops 5242880 | bytes 12593152 | tf_op jit(solution)/shard_map/add | solution.py:51
  69.4 8.5 %fusion.32 = f32[1024,128]{1,0:T(8,128)S(1)} fusion(f32[1024,1024]{0,1:T(8,128)S(1)} %fusion), kind=kOutput, calls=%fused_computation.69 | convolution fusion | flops 1612447744 | bytes 4718592 | tf_op jit(solution)/shard_map/dot_general | solution.py:30
  77.9 21.3 %convolution_negate_fusion = f32[1024,128]{1,0:T(8,128)S(1)} fusion(f32[1024,1024]{0,1:T(8,128)S(1)} %fusion), kind=kOutput, calls=%fused_computation.14 | convolution fusion | flops 1612578816 | bytes 4718592 | tf_op jit(solution)/shard_map/dot_general | solution.py:30
  99.2 8.6 %gather_fusion = f32[1024,1024]{1,0:T(8,128)} fusion(f32[1024,1024]{0,1:T(8,128)} %get-tuple-element.7, s32[1024]{0:T(1024)S(1)} %get-tuple-element.29), kind=kCustom, calls=%fused_computation.clone | custom fusion | bytes 8392704 | tf_op jit(solution)/shard_map/jit(_take)/gather | solution.py:49
  107.8 8.6 %gather_fusion.1 = f32[1024,1024]{1,0:T(8,128)} fusion(f32[1024,1024]{0,1:T(8,128)} %get-tuple-element.7, s32[1024]{0:T(1024)S(1)} %get-tuple-element.30), kind=kCustom, calls=%fused_computation.1.clone | custom fusion | bytes 8392704 | tf_op jit(solution)/shard_map/jit(_take)/gather | solution.py:50
  116.4 4.0 %fusion.1 = f32[1024,1024]{0,1:T(8,128)S(1)} fusion(f32[1024,1024]{1,0:T(8,128)} %gather_fusion.1, f32[1024,1024]{1,0:T(8,128)} %gather_fusion, f32[1024]{0:T(1024)S(1)} %bitcast.250, f32[1024]{0:T(1024)S(1)} %bitcast.249, pred[1024]{0:T(1024)(128)(4,1)S(1)} %get-tuple-element.28, pred[1024]{0:T(1024)(128)(4,1)S(1)} %get-tuple-element.27), kind=kLoop, calls=%fused_computation.10 | loop fusion | flops 5242880 | bytes 12593152 | tf_op jit(solution)/shard_map/add | solution.py:51
  120.4 8.5 %fusion.34 = f32[1024,128]{1,0:T(8,128)S(1)} fusion(f32[1024,1024]{0,1:T(8,128)S(1)} %fusion.1), kind=kOutput, calls=%fused_computation.70 | convolution fusion | flops 1612447744 | bytes 4718592 | tf_op jit(solution)/shard_map/dot_general | solution.py:30
  128.9 8.9 %convolution_negate_fusion.1 = f32[1024,128]{1,0:T(8,128)S(1)} fusion(f32[1024,1024]{0,1:T(8,128)S(1)} %fusion.1), kind=kOutput, calls=%fused_computation.15 | convolution fusion | flops 1612578816 | bytes 4718592 | tf_op jit(solution)/shard_map/dot_general | solution.py:30
  137.9 3.0 fusion.42
  140.9 3.0 fusion.40
  143.9 3.0 fusion.3
  146.9 3.0 fusion.2
  149.9 3.0 fusion.46
  152.9 3.2 fusion.44
  156.1 3.0 fusion.5
  159.1 3.0 fusion.4
  168.7 47.5 %all-gather.3.cloned.1.call-done = f32[32,2,128,128]{3,2,1,0:T(8,128)} async-done(((f32[2,2,128,128]{3,2,1,0:T(8,128)}), f32[32,2,128,128]{3,2,1,0:T(8,128)}) %all-gather.3.cloned.1.call-update) | async-done | bytes 4194320 | tf_op jit(solution)/shard_map/all_gather | solution.py:13
  218.6 89.5 %all-reduce.4.cloned.1.call-done = (f32[2,128,128]{2,1,0:T(8,128)}, f32[2,128,128]{2,1,0:T(8,128)}) async-done(((f32[2,128,128]{2,1,0:T(8,128)}, f32[2,128,128]{2,1,0:T(8,128)}), (f32[2,128,128]{2,1,0:T(8,128)}, f32[2,128,128]{2,1,0:T(8,128)})) %all-reduce.4.cloned.1.call-update) | async-done | bytes 262160 | tf_op jit(solution)/shard_map/psum | solution.py:20
  319.8 32.4 %pmax.7 = f32[2]{0:T(128)} all-reduce(f32[2]{0:T(128)S(1)} %pad_maximum_fusion.2), channel_id=1, replica_groups=mesh['grp'=2,'slab'=16] {'slab'}, use_global_device_ids=true, to_apply=%region_9.11 | all-reduce | flops 2 | bytes 16 | tf_op jit(solution)/shard_map/pmax | solution.py:128
  (45 shorter events, 19.9 us)
Async XLA Ops:
  7.2 209.0 %all-gather.3.cloned.1.call-start = ((), (), s32[]{:S(2)}) async-start(), calls=%async_computation | async-start | bytes 4456448 | tf_op jit(solution)/shard_map/all_gather | solution.py:13
  56.4 8.6 %copy-start.1 = (f32[2,1024]{1,0:T(2,128)S(1)}, f32[2,1024]{1,0:T(2,128)}, u32[]{:S(2)}) copy-start(f32[2,1024]{1,0:T(2,128)} %param.14) | copy-start | bytes 24580
  152.9 10.0 %copy-start.3 = (s32[16]{0:T(128)S(1)}, s32[16]{0:T(128)}, u32[]{:S(2)}) copy-start(s32[16]{0:T(128)} %param.16) | copy-start | bytes 196
  152.9 11.9 %copy-start = (f32[1,2,128,128]{3,2,1,0:T(8,128)S(1)}, f32[1,2,128,128]{3,2,1,0:T(8,128)}, u32[]{:S(2)}) copy-start(f32[1,2,128,128]{3,2,1,0:T(8,128)} %param.17) | copy-start | bytes 393220
  152.9 12.7 %copy-start.2 = (s32[2,2]{1,0:T(2,128)S(1)}, s32[2,2]{1,0:T(2,128)}, u32[]{:S(2)}) copy-start(s32[2,2]{1,0:T(2,128)} %param.15) | copy-start | bytes 52
  162.8 145.3 %all-reduce.4.cloned.1.call-start = ((), (), s32[]{:S(2)}) async-start(), calls=%async_computation.1 | async-start | bytes 524288 | tf_op jit(solution)/shard_map/psum | solution.py:20
Sparse Core Ops, SparseCore 0:
  163.0 53.1 all-gather.2
  219.6 88.4 all-reduce.3
